TPU v7x, 512 devices: a 8x2x16 block of a 8x8x16 slice. The times are simulated.
512 devices in a mesh: parts: 2 (over y), seq: 256 (over x, z, core).
Axes of the slice: x: 8, y: 2, z: 16, core: 2. Of those that a mesh axis runs over, the one named last changes fastest.
The devices are a block of a 8x8x16 slice.
Arguments:
- queries: bfloat16 [8, 8192], P('parts', 'seq'), parts along dimension 0
- new_kv: bfloat16 [8, 2048], P('parts', 'seq'), parts along dimension 0, may hold values from -6 to 6
- keys: bfloat16 [1024, 512, 1024], P(('parts', 'seq')), parts along dimension 0, may hold values from -6 to 6
- values: bfloat16 [1024, 512, 1024], P(('parts', 'seq')), parts along dimension 0, may hold values from -6 to 6
- slot_request: int32 [1024], P(('parts', 'seq')), parts along dimension 0, may hold values from 0 to 3, as said below
- slot_length: int32 [1024], P(('parts', 'seq')), parts along dimension 0, may hold values from 1 to 512
Outputs:
- attended: bfloat16 [8, 8192], P('parts'), parts along dimension 0
There are 2 independent parts, one for each index of `parts`. A program takes and returns all parts, laid end to end along the dimension named above; each array names one. Nothing has to cross between parts.
Inputs may be any that keep to these rules, and one draw needn't show every extreme that they name: `slot_request`: every request number 0 to 3 owns at least one block.
All inputs are finite; a program needn't handle non-finite values.
Results may differ from a plain program's by a relative error of at most 0.0055.
Values may be sent and summed in bfloat16 or wider, within the bound.
A program may use at most 128 MiB of HBM per device.

v0:
```python
import jax
import jax.numpy as jnp
from jax import lax
from jax.sharding import Mesh
from jax.sharding import PartitionSpec as P

H = 64
KVH = 8
DH = 128
SEQ = ("seq_0", "seq_1", "seq_2")
PARTS_SEQ = ("parts", "seq_0", "seq_1", "seq_2")


very_negative = -1e30


def joined_along(tiles, dim):
    tiles = jnp.moveaxis(tiles, 0, dim)
    dims = tiles.shape
    return tiles.reshape(*dims[:dim], dims[dim] * dims[dim + 1], *dims[dim + 2 :])


def gather_in_order(x, axes, turns):
    tiles = x
    for k in turns:
        tiles = lax.all_gather(tiles, axes[k])
    done = turns[::-1]
    back = [done.index(k) for k in range(len(axes))]
    tiles = tiles.transpose(*back, *range(len(axes), tiles.ndim))
    return tiles.reshape(-1, *x.shape)


def gather_axes(x, axes, turns, dim):
    return joined_along(gather_in_order(x, axes, turns), dim)


def all_in_one(x, axis):
    leaves = jax.tree.leaves(x)
    turns = sorted(range(len(leaves)), key=lambda k: -leaves[k].size)
    width = (1, *leaves[turns[0]].shape)[-1]
    lines = [
        jnp.pad(leaves[k].reshape(-1), (0, -leaves[k].size % width)).reshape(-1, width)
        for k in turns
    ]
    both, at, found = (lax.all_gather(jnp.concatenate(lines), axis), 0, {})
    for k, line in zip(turns, lines):
        share = both[:, at : at + len(line)].reshape(len(both), -1)
        found[k] = share[:, : leaves[k].size].reshape(-1, *leaves[k].shape)
        at += len(line)
    numbers = iter(range(len(leaves)))
    return jax.tree.map(lambda _: found[next(numbers)], x)


def merged_by_axis(x, axes, combine):
    for axis in axes:
        pieces = all_in_one(x, axis)
        x = jax.tree.map(lambda part: part[0], pieces)
        for k in range(1, lax.axis_size(axis)):
            x = combine(x, jax.tree.map(lambda part: part[k], pieces))
    return x


def combine_parts(first, second):
    top_first, sum_first, out_first = first
    top_second, sum_second, out_second = second
    peak = jnp.maximum(top_first, top_second)
    weight_first = jnp.exp(top_first - peak)
    weight_second = jnp.exp(top_second - peak)
    summed = sum_first * weight_first + sum_second * weight_second
    outputs = out_first * weight_first[..., None] + out_second * weight_second[..., None]
    return (peak, summed, outputs)


def shards(queries, new_kv, keys, values, slot_request, slot_length):
    all_queries, all_new = (
        gather_axes(queries, SEQ, (0, 1, 2), 1),
        gather_axes(new_kv, SEQ, (0, 1, 2), 1),
    )
    requests = all_queries.shape[0]
    group_size = H // KVH
    score_scale = DH ** (-0.5)
    query_heads = all_queries.reshape(requests, KVH, group_size, DH)
    slot_count = keys.shape[0]
    block_len = keys.shape[1]
    owner = slot_request[:, None] == jnp.arange(requests, dtype=jnp.int32)[None, :]
    picked = jnp.einsum(
        "sr,rkgd->skgd", owner.astype(jnp.bfloat16), query_heads, preferred_element_type=jnp.float32
    ).astype(jnp.bfloat16)
    key_tiles = keys.reshape(slot_count, block_len, KVH, DH)
    value_tiles = values.reshape(slot_count, block_len, KVH, DH)
    scores = (
        jnp.einsum("skgd,stkd->skgt", picked, key_tiles, preferred_element_type=jnp.float32)
        * score_scale
    )
    inside = jnp.arange(block_len, dtype=jnp.int32)[None, :] < slot_length[:, None]
    scores = jnp.where(inside[:, None, None, :], scores, very_negative)
    slot_top = jnp.max(scores, axis=-1)
    weights = jnp.exp(scores - slot_top[..., None])
    slot_sum = jnp.sum(weights, axis=-1)
    slot_out = jnp.einsum(
        "skgt,stkd->skgd",
        weights.astype(jnp.bfloat16),
        value_tiles,
        preferred_element_type=jnp.float32,
    )
    owner_wide = owner[:, :, None, None]
    dense_top = jnp.max(jnp.where(owner_wide, slot_top[:, None], very_negative), axis=0)
    factor = jnp.where(owner_wide, jnp.exp(slot_top[:, None] - dense_top[None]), 0.0)
    dense_sum = jnp.sum(factor * slot_sum[:, None], axis=0)
    dense_out = jnp.einsum("srkg,skgd->rkgd", factor, slot_out, precision=lax.Precision.HIGHEST)
    total_top, total_sum, total_out = merged_by_axis(
        (dense_top, dense_sum, dense_out), SEQ, combine_parts
    )
    new_pair = all_new.astype(jnp.float32).reshape(requests, 2, KVH, DH)
    new_score = (
        jnp.einsum("rkgd,rkd->rkg", query_heads.astype(jnp.float32), new_pair[:, 0]) * score_scale
    )
    peak = jnp.maximum(total_top, new_score)
    old_weight = jnp.exp(total_top - peak)
    new_weight = jnp.exp(new_score - peak)
    rounded_new = new_weight.astype(jnp.bfloat16).astype(jnp.float32)
    numer = (
        total_out * old_weight[..., None] + rounded_new[..., None] * new_pair[:, 1][:, :, None, :]
    )
    denom = total_sum * old_weight + new_weight
    attended = numer / denom[..., None]
    return attended.reshape(requests, H * DH).astype(jnp.bfloat16)


def solution(mesh):
    torus = Mesh(
        mesh.devices.reshape(mesh.shape["parts"], 8, 16, 2), ("parts", "seq_0", "seq_1", "seq_2")
    )
    placed = (
        P("parts", SEQ),
        P("parts", SEQ),
        P(PARTS_SEQ, None, None),
        P(PARTS_SEQ, None, None),
        P(PARTS_SEQ),
        P(PARTS_SEQ),
    )
    return jax.shard_map(
        shards, mesh=torus, in_specs=placed, out_specs=P("parts", None), check_vma=False
    )
```

profile of v0, /device:TPU:65, one launch (start us, length us, event | category | flops | bytes accessed | tf_op | source)
XLA Modules:
  0.0 240.4 jit_solution(18292940494160735934)
XLA Ops:
  6.5 0.0 copy-start
  6.6 0.0 all-gather.17.cloned.1.call-start
  6.6 0.9 iota_compare_fusion.1
  7.4 0.7 iota_compare_fusion
  8.2 14.4 %all-gather.9 = bf16[8,4,32]{2,1,0:T(4,128)(2,1)S(1)} all-gather(bf16[1,4,32]{2,1,0:T(4,128)(2,1)} %bitcast.1167), channel_id=2, replica_groups=mesh['parts'=2,'seq_0'=8,'seq_1'=16,'seq_2'=2] {'seq_0'}, dimensions={0}, use_global_device_ids=true | all-gather | bytes 2304 | tf_op jit(solution)/shard_map/all_gather | solution.py:26
  22.6 61.4 %all-gather.1 = bf16[128,4,32]{2,1,0:T(4,128)(2,1)S(1)} all-gather(bf16[8,4,32]{2,1,0:T(4,128)(2,1)S(1)} %all-gather.9), channel_id=3, replica_groups=mesh['parts'=2,'seq_0'=8,'seq_1'=16,'seq_2'=2] {'seq_1'}, dimensions={0}, use_global_device_ids=true | all-gather | bytes 34816 | tf_op jit(solution)/shard_map/all_gather | solution.py:26
  84.1 13.3 %all-gather.2 = bf16[32,8,4,32]{3,1,2,0:T(8,128)(2,1)S(1)} all-gather(bf16[16,8,4,32]{3,1,2,0:T(8,128)(2,1)S(1)} %copy.39), channel_id=4, replica_groups=mesh['parts'=2,'seq_0'=8,'seq_1'=16,'seq_2'=2] {'seq_2'}, dimensions={0}, use_global_device_ids=true | all-gather | bytes 98304 | tf_op jit(solution)/shard_map/all_gather | solution.py:26
  97.4 0.3 copy.40
  97.6 0.2 reshape_reshape.2
  97.8 0.9 convolution_convert_fusion
  98.7 0.0 copy-done
  98.7 0.7 fusion.252
  99.4 0.1 copy.45
  99.6 0.2 fusion.12
  99.8 2.0 fusion
  101.8 0.0 copy-start.1
  101.8 0.1 copy.49
  101.9 0.2 select_reduce_fusion
  102.1 0.1 copy.48
  102.2 0.2 multiply_reduce_fusion
  102.5 0.1 copy.50
  102.6 0.1 reshape.1702
  102.7 0.1 reshape.1701
  102.8 0.9 convolution_bitcast_fusion
  103.7 0.7 maximum_bitcast_fusion
  104.3 0.1 all-gather.17.cloned.1.call-update
  104.4 0.1 all-gather.19.cloned.1.call-start
  104.5 30.1 %all-gather.17.cloned.1.call-done = f32[8,260,128]{2,1,0:T(8,128)} async-done(((f32[1,260,128]{2,1,0:T(8,128)}), f32[8,260,128]{2,1,0:T(8,128)}) %all-gather.17.cloned.1.call-update) | async-done | bytes 1064976 | tf_op jit(solution)/shard_map/all_gather | solution.py:45
  134.6 0.7 fusion.211
  135.3 0.8 fusion.146
  136.1 0.7 fusion.210
  136.8 0.7 fusion.208
  137.5 0.7 fusion.206
  138.2 1.8 fusion.62
  140.1 0.7 maximum_bitcast_fusion.1
  140.7 0.1 all-gather.19.cloned.1.call-update
  140.8 0.0 copy-done.1
  140.8 11.7 %all-gather.13 = bf16[8,4,8]{2,1,0:T(4,128)(2,1)S(1)} all-gather(bf16[1,4,8]{2,1,0:T(4,128)(2,1)S(1)} %bitcast.1168), channel_id=8, replica_groups=mesh['parts'=2,'seq_0'=8,'seq_1'=16,'seq_2'=2] {'seq_0'}, dimensions={0}, use_global_device_ids=true | all-gather | bytes 576 | tf_op jit(solution)/shard_map/all_gather | solution.py:26
  152.5 25.3 %all-gather.7 = bf16[128,4,8]{2,1,0:T(4,128)(2,1)S(1)} all-gather(bf16[8,4,8]{2,1,0:T(4,128)(2,1)S(1)} %all-gather.13), channel_id=9, replica_groups=mesh['parts'=2,'seq_0'=8,'seq_1'=16,'seq_2'=2] {'seq_1'}, dimensions={0}, use_global_device_ids=true | all-gather | bytes 8704 | tf_op jit(solution)/shard_map/all_gather | solution.py:26
  177.8 17.2 %all-gather.8 = bf16[32,8,4,8]{3,1,2,0:T(8,128)(2,1)S(1)} all-gather(bf16[16,8,4,8]{3,1,2,0:T(8,128)(2,1)S(1)} %copy.51), channel_id=10, replica_groups=mesh['parts'=2,'seq_0'=8,'seq_1'=16,'seq_2'=2] {'seq_2'}, dimensions={0}, use_global_device_ids=true | all-gather | bytes 24576 | tf_op jit(solution)/shard_map/all_gather | solution.py:26
  195.0 0.3 copy.58
  195.3 0.2 reshape.1704
  195.5 0.1 fusion.92
  195.7 15.0 %all-gather.19.cloned.1.call-done = f32[16,260,128]{2,1,0:T(8,128)} async-done(((f32[1,260,128]{2,1,0:T(8,128)}), f32[16,260,128]{2,1,0:T(8,128)}) %all-gather.19.cloned.1.call-update) | async-done | bytes 2129936 | tf_op jit(solution)/shard_map/all_gather | solution.py:45
  210.7 0.7 fusion.196
  211.4 0.9 fusion.101
  212.3 0.7 fusion.195
  213.0 0.7 fusion.193
  213.7 0.7 fusion.191
  214.4 0.7 fusion.189
  215.1 0.7 fusion.187
  215.8 0.7 fusion.185
  216.5 0.7 fusion.183
  217.2 2.6 %fusion.17 = f32[256,128]{1,0:T(8,128)S(1)} fusion(f32[16,260,128]{2,1,0:T(8,128)} %all-gather.19.cloned.1.call-done, f32[256]{0:T(256)S(1)} %get-tuple-element.67, f32[256]{0:T(256)S(1)} %get-tuple-element.64, f32[256]{0:T(256)S(1)} %get-tuple-element.66, f32[256]{0:T(256)S(1)} %get-tuple-element.65, f32[256]{0:T(256)S(1)} %get-tuple-element.63, ...), kind=kLoop, calls=%fused_computation.24 | loop fusion | flops 1474560 | bytes 2258944 | tf_op jit(solution)/shard_map/add | solution.py:70
  219.9 11.8 %all-gather.12 = f32[2,260,128]{2,1,0:T(8,128)S(1)} all-gather(f32[1,260,128]{2,1,0:T(8,128)S(1)} %maximum_bitcast_fusion.2), channel_id=7, replica_groups=mesh['parts'=2,'seq_0'=8,'seq_1'=16,'seq_2'=2] {'seq_2'}, dimensions={0}, use_global_device_ids=true | all-gather | bytes 399360 | tf_op jit(solution)/shard_map/all_gather | solution.py:45
  231.7 0.1 squeeze.383
  231.8 0.1 squeeze.386
  231.9 0.1 squeeze.382
  232.0 0.1 squeeze.387
  232.1 0.1 broadcast_bitcast_fusion.3
  232.2 0.1 squeeze.384
  232.3 0.1 broadcast_bitcast_fusion.1
  232.4 0.1 multiply_bitcast_fusion
  232.5 1.0 fusion.83
  (9 shorter events, 0.2 us)
Async XLA Ops:
  6.5 92.2 %copy-start = (bf16[2,512,1024]{2,1,0:T(8,128)(2,1)S(1)}, bf16[2,512,1024]{2,1,0:T(8,128)(2,1)}, u32[]{:S(2)}) copy-start(bf16[2,512,1024]{2,1,0:T(8,128)(2,1)} %param.8) | copy-start | bytes 6291460
  6.6 128.1 %all-gather.17.cloned.1.call-start = ((), (), s32[]{:S(2)}) async-start(), calls=%async_computation | async-start | bytes 1216512 | tf_op jit(solution)/shard_map/all_gather | solution.py:45
  101.8 39.0 %copy-start.1 = (bf16[4,8]{1,0:T(4,128)(2,1)S(1)}, bf16[4,8]{1,0:T(4,128)(2,1)}, u32[]{:S(2)}) copy-start(bf16[4,8]{1,0:T(4,128)(2,1)} %param.7) | copy-start | bytes 196
  104.4 106.3 %all-gather.19.cloned.1.call-start = ((), (), s32[]{:S(2)}) async-start(), calls=%async_computation.1 | async-start | bytes 2297856 | tf_op jit(solution)/shard_map/all_gather | solution.py:45
Sparse Core Ops, SparseCore 0:
  104.5 30.0 all-gather.16
  140.9 69.7 all-gather.18
where the time goes:
time: 241 us; the launch traced here: 240 us
  blocking collectives  155 us (64%)
  waiting for transfers between devices  45.2 us (19%)
  other arithmetic  19.3 us (8%)
  between operations  13.6 us (6%)
  matrix products  4.7 us (2%)
    all_gather x6, blocking collectives, gather_in_order(): tiles = lax.all_gather(tiles, axes[k])  143 us
    all_gather x2, waiting for transfers between devices, all_in_one(): both, at, found = (lax.all_gather(jnp.concatenate(lines), axis), 0, {})  45.1 us
    all_gather x1, blocking collectives, all_in_one(): both, at, found = (lax.all_gather(jnp.concatenate(lines), axis), 0, {})  11.8 us
    exp x10, other arithmetic, combine_parts(): weight_second = jnp.exp(top_second - peak)  7.04 us
  transfers between devices with their start and end apart: 2, of which 2 were waited for; matrix products, arithmetic and copies ran while one was open for 0% of the time, Pallas kernels for 0%

commit v1 on v0

v1 whole, which is shorter than its diff:
```python
import functools

import jax
import jax.numpy as jnp
from jax import lax
from jax.experimental import pallas as pl
from jax.experimental.pallas import tpu as pltpu
from jax.sharding import Mesh
from jax.sharding import PartitionSpec as P

H = 64
KVH = 8
DH = 128
G = H // KVH
LANES = 128
NX, NZ, NC = 8, 16, 2
AX, AZ, AC = "seq_0", "seq_1", "seq_2"
SEQ = (AX, AZ, AC)
PARTS_SEQ = ("parts", AX, AZ, AC)
NEG = -1e30
MESH = pl.DeviceIdType.MESH
F32, BF16 = jnp.float32, jnp.bfloat16
FAR_X = (4, 3, 5, 2, 6, 1, 7)
FAR_Z = (8, 7, 9, 6, 10, 5, 11, 4, 12, 3, 13, 2, 14, 1, 15)


def iota(shape, dim):
    return lax.broadcasted_iota(jnp.int32, shape, dim)


def at(x, z, c):
    return {AX: x, AZ: z, AC: c}


def wait_for(ref, sem):
    pltpu.make_async_copy(ref, ref, sem).wait()


def kernel(
    req_ref, len_ref, q_ref, kv_ref, k_hbm, v_hbm, out_ref,
    kbuf, vbuf, buf1, g2, kv2, qscr, so, sml, ro, rml, ao, aml,
    load_sem, send_sem, recv_sem, z_sem,
):
    x, z, c = lax.axis_index(AX), lax.axis_index(AZ), lax.axis_index(AC)
    requests, width = q_ref.shape
    new_width = kv_ref.shape[1]
    slots, block = k_hbm.shape[0], k_hbm.shape[1]
    xc = NX * NC
    zh, zl = z // 2, z % 2
    mine_d = zl * NC + c
    mine = x * 4 + mine_d
    scale = DH**-0.5

    barrier = pltpu.get_barrier_semaphore()
    for dx in range(NX):
        for dc in range(NC):
            if dx or dc:
                pl.semaphore_signal(
                    barrier, 1, device_id=at((x + dx) % NX, z, (c + dc) % NC), device_id_type=MESH
                )
    near = (1, 2, 3, 4, NZ - 4, NZ - 3, NZ - 2, NZ - 1)
    for dz in near:
        pl.semaphore_signal(barrier, 1, device_id=at(x, (z + dz) % NZ, c), device_id_type=MESH)

    loads = []
    for s in range(slots):
        loads.append(pltpu.make_async_copy(k_hbm.at[s], kbuf.at[s], load_sem.at[s]))
    for s in range(slots):
        loads.append(pltpu.make_async_copy(v_hbm.at[s], vbuf.at[s], load_sem.at[slots + s]))
    for load in loads:
        load.start()

    def as_row(ref, n):
        spread = (iota((n, LANES), 0) == iota((n, LANES), 1) % n).astype(BF16)
        wide = jnp.dot(ref[...], spread, preferred_element_type=F32)
        keep = iota((requests, LANES), 0) == iota((requests, LANES), 1) // n
        return jnp.sum(jnp.where(keep, wide, 0.0), axis=0, keepdims=True)

    row1 = c * NX + x
    buf1[pl.ds(row1, 1), :, 0:LANES] = as_row(q_ref, width)[None]
    buf1[pl.ds(row1, 1), :, LANES : 2 * LANES] = as_row(kv_ref, new_width)[None]

    req = [req_ref[s] for s in range(slots)]
    length = [len_ref[s] for s in range(slots)]
    lane512 = iota((LANES, 2 * NC * LANES), 1)
    sub512 = iota((LANES, 2 * NC * LANES), 0)
    place = []
    for zp in range(2):
        m = lane512 % LANES
        want = jnp.where((lane512 // LANES) % 2 == 0, req[0], req[1]) * width + m % width
        piece = zp * NC + lane512 // (2 * LANES)
        place.append(((sub512 == want) & (m // width == piece)).astype(BF16))

    pl.semaphore_wait(barrier, xc - 1 + len(near))
    for there in (at(x, (z + 4) % NZ, c), at(x, (z + NZ - 4) % NZ, c), at(x, 2 * zh + 1 - zl, c)):
        pl.semaphore_signal(z_sem, 1, device_id=there, device_id_type=MESH)

    def send(src, dst, phase, there):
        pltpu.make_async_remote_copy(
            src_ref=src,
            dst_ref=dst,
            send_sem=send_sem.at[phase],
            recv_sem=recv_sem.at[phase],
            device_id=there,
            device_id_type=MESH,
        ).start()

    for dx in FAR_X + (0,):
        for dc in range(NC):
            if dx or dc:
                send(buf1.at[row1], buf1.at[row1], 0, at((x + dx) % NX, z, (c + dc) % NC))
    wait_for(buf1.at[pl.ds(0, xc - 1)], recv_sem.at[0])
    rows = buf1[:, 0, :]
    g2[pl.ds(z, 1)] = rows[:, 0:LANES].astype(BF16)[None]
    kv2[pl.ds(z, 1)] = rows[:, LANES : 2 * LANES].astype(BF16)[None]

    pl.semaphore_wait(z_sem, 3)
    for dz in FAR_Z:
        send(g2.at[z], g2.at[z], 1, at(x, (z + dz) % NZ, c))
    for dz in FAR_Z:
        send(kv2.at[z], kv2.at[z], 2, at(x, (z + dz) % NZ, c))
    for load in loads:
        load.wait()
    wait_for(g2.at[pl.ds(0, NZ - 1)], recv_sem.at[1])

    picked = [None, None]
    for zp in range(2):
        lhs = jnp.concatenate([g2[2 * i + zp] for i in range(G)], axis=0)
        placed = jnp.dot(lhs, place[zp], preferred_element_type=F32).reshape(G, xc, 2 * NC * LANES)
        for s in range(slots):
            for cc in range(NC):
                at_lane = (cc * 2 + s) * LANES
                part = placed[:, cc * NX : (cc + 1) * NX, at_lane : at_lane + LANES]
                picked[s] = part if picked[s] is None else picked[s] + part
    for s in range(slots):
        qscr[s] = picked[s]

    lane = iota((G, LANES), 1)
    lane_s, lane_hh, lane_r = (lane // 8) % 2, (lane // 4) % 2, lane % 4
    inside = [iota((G, block), 1) < length[s] for s in range(slots)]
    order = FAR_X + (0,)
    weights, vals = {}, {}
    for n, dx in enumerate(order):
        k = (x + dx) % NX
        cols = pl.ds(pl.multiple_of(k * DH, DH), DH)
        tops, sums = [], []
        for s in range(slots):
            qk = qscr[s, :, k, :].astype(BF16)
            sc = lax.dot_general(
                qk, kbuf[s, :, cols], (((1,), (1,)), ((), ())), preferred_element_type=F32
            )
            sc = jnp.where(inside[s], sc * scale, NEG)
            top = jnp.max(sc, axis=1, keepdims=True)
            w = jnp.exp(sc - top)
            tops.append(top)
            sums.append(jnp.sum(w, axis=1, keepdims=True))
            weights[n, s] = w.astype(BF16)
        of_slot = [
            jnp.where(
                lane < 64,
                jnp.where(lane_r == req[s], tops[s], NEG),
                jnp.where(lane_r == req[s], sums[s], 0.0),
            )
            for s in range(slots)
        ]
        vals[n] = jnp.where(lane_s == 0, of_slot[0], of_slot[1])
    for n, dx in enumerate(order):
        k = (x + dx) % NX
        cols = pl.ds(pl.multiple_of(k * DH, DH), DH)
        for d in range(4):
            sml[n, d] = jnp.where(
                lane_hh[0:1] == 0, vals[n][2 * d : 2 * d + 1], vals[n][2 * d + 1 : 2 * d + 2]
            )
        for s in range(slots):
            o = jnp.dot(weights[n, s], vbuf[s, :, cols], preferred_element_type=F32)
            for d in range(4):
                so[n, d, 2 * s : 2 * s + 2, :] = o[2 * d : 2 * d + 2]
        for dd in range(4):
            if dx or dd:
                d = dd if dx else (mine_d + dd) % 4
                there = at(k, 2 * zh + d // NC, d % NC)
                send(sml.at[n, d], rml.at[mine], 4, there)
                send(so.at[n, d], ro.at[mine], 3, there)
    last = len(order) - 1
    ro[pl.ds(mine, 1)] = so[last, pl.ds(mine_d, 1)]
    rml[pl.ds(mine, 1)] = sml[last, pl.ds(mine_d, 1)]

    wait_for(kv2.at[pl.ds(0, NZ - 1)], recv_sem.at[2])
    total_rows = NZ * xc
    u, col = iota((2 * xc, total_rows), 0), iota((2 * xc, total_rows), 1)
    source = (
        ((x % 2) * (NZ // 2) + (u % xc) // NC) * xc + (u % NC) * NX + x // 2 + (NX // 2) * (u // xc)
    )
    pick = (col == source).astype(BF16)
    new = jnp.dot(pick, kv2[...].reshape(total_rows, LANES), preferred_element_type=F32)
    wide_l, wide_m = iota((LANES, requests * LANES), 0), iota((LANES, requests * LANES), 1)
    wide_r, wide_m = wide_m // LANES, wide_m % LANES
    to_new = (wide_l == wide_r * new_width + wide_m % new_width).astype(BF16)
    to_q = (wide_l == wide_r * width + wide_m % width).astype(BF16)
    new = jnp.dot(new.astype(BF16), to_new, preferred_element_type=F32)
    keep = (iota(new.shape, 1) % LANES) // new_width == iota(new.shape, 0) % xc
    new = jnp.where(keep, new, 0.0)

    def by_request(flat):
        return [flat[:, r * LANES : (r + 1) * LANES] for r in range(requests)]

    new_k = by_request(jnp.sum(new[0:xc], axis=0, keepdims=True))
    new_v = by_request(jnp.sum(new[xc : 2 * xc], axis=0, keepdims=True))
    u, col = iota((8, total_rows), 0), iota((8, total_rows), 1)
    member = 2 * mine_d + u // 4
    source = (2 * member + (u % 4) // NC) * xc + (u % NC) * NX + x
    pick = (col == source).astype(BF16)
    own_q = jnp.dot(pick, g2[...].reshape(total_rows, LANES), preferred_element_type=F32)
    own_q = jnp.dot(own_q.astype(BF16), to_q, preferred_element_type=F32)
    keep = (iota(own_q.shape, 1) % LANES) // width == iota(own_q.shape, 0) % 4
    own_q = jnp.where(keep, own_q, 0.0)
    q_rows = by_request(jnp.sum(own_q[0:4], axis=0, keepdims=True)) + by_request(
        jnp.sum(own_q[4:8], axis=0, keepdims=True)
    )
    q_rows = jnp.concatenate(q_rows, axis=0)
    k_rows = jnp.concatenate(new_k + new_k, axis=0)
    v_rows = jnp.concatenate(new_v + new_v, axis=0)
    new_score = jnp.sum(q_rows * k_rows, axis=1, keepdims=True) * scale

    group = 4 * NX
    wait_for(rml.at[pl.ds(0, group - 1)], recv_sem.at[4])
    ml = rml[:, 0, :]
    top = jnp.max(ml, axis=0, keepdims=True)
    top = jnp.maximum(top, pltpu.roll(top, 8, 1))
    w = jnp.exp(ml - top)
    total = jnp.sum(w * pltpu.roll(ml, 64, 1), axis=0, keepdims=True)
    total = total + pltpu.roll(total, 8, 1)
    lane1 = iota((1, LANES), 1)
    aml[pl.ds(zh, 1)] = jnp.where(lane1 < 64, top, pltpu.roll(total, 64, 1))[None]
    wait_for(ro.at[pl.ds(0, group - 1)], recv_sem.at[3])
    merged = []
    for hh in range(2):
        planes = [ro[:, s * 2 + hh, :] for s in range(slots)]
        for r in range(requests):
            acc = None
            for s in range(slots):
                i = 16 + s * 8 + hh * 4 + r
                part = w[:, i : i + 1] * planes[s]
                acc = part if acc is None else acc + part
            merged.append(jnp.sum(acc, axis=0, keepdims=True))
    ao[pl.ds(zh, 1)] = jnp.concatenate(merged, axis=0)[None]

    for dz in FAR_X:
        there = at(x, 2 * ((zh + dz) % NX) + zl, c)
        send(aml.at[zh], aml.at[zh], 6, there)
        send(ao.at[zh], ao.at[zh], 5, there)
    pairs = NZ // 2
    wait_for(aml.at[pl.ds(0, pairs - 1)], recv_sem.at[6])
    sub = iota((8, LANES), 0)
    lane8 = iota((8, LANES), 1)
    m_at, l_at = lane8 == 16 + sub, lane8 == 80 + sub
    ms = [jnp.sum(jnp.where(m_at, aml[i], 0.0), axis=1, keepdims=True) for i in range(pairs)]
    ls = [jnp.sum(jnp.where(l_at, aml[i], 0.0), axis=1, keepdims=True) for i in range(pairs)]
    peak = functools.reduce(jnp.maximum, ms, new_score)
    new_w = jnp.exp(new_score - peak)
    factors = [jnp.exp(m - peak) for m in ms]
    denom = new_w
    for i in range(pairs):
        denom = denom + factors[i] * ls[i]
    wait_for(ao.at[pl.ds(0, pairs - 1)], recv_sem.at[5])
    numer = new_w * v_rows
    for i in range(pairs):
        numer = numer + factors[i] * ao[i]
    final = (numer / denom).astype(BF16)

    base = pl.multiple_of(mine * 2 * DH, 2 * DH)
    out_ref[:, pl.ds(base, DH)] = final[0:4]
    out_ref[:, pl.ds(pl.multiple_of(base + DH, DH), DH)] = final[4:8]
    here = out_ref.at[:, pl.ds(base, 2 * DH)]
    for dx in FAR_X + (0,):
        for dd in range(4):
            if dx or dd:
                d = (mine_d + dd) % 4
                send(here, here, 7, at((x + dx) % NX, 2 * zh + d // NC, d % NC))
    wait_for(out_ref.at[:, pl.ds(0, (group - 1) * 2 * DH)], recv_sem.at[7])

    wait_for(buf1.at[pl.ds(0, xc - 1)], send_sem.at[0])
    wait_for(g2.at[pl.ds(0, NZ - 1)], send_sem.at[1])
    wait_for(kv2.at[pl.ds(0, NZ - 1)], send_sem.at[2])
    wait_for(ro.at[pl.ds(0, group - 1)], send_sem.at[3])
    wait_for(rml.at[pl.ds(0, group - 1)], send_sem.at[4])
    wait_for(ao.at[pl.ds(0, pairs - 1)], send_sem.at[5])
    wait_for(aml.at[pl.ds(0, pairs - 1)], send_sem.at[6])
    wait_for(out_ref.at[:, pl.ds(0, (group - 1) * 2 * DH)], send_sem.at[7])


def shards(queries, new_kv, keys, values, slot_request, slot_length):
    slots, block, columns = keys.shape
    requests = queries.shape[0]
    xc, group = NX * NC, 4 * NX
    smem = pl.BlockSpec(memory_space=pltpu.SMEM)
    vmem = pl.BlockSpec(memory_space=pltpu.VMEM)
    hbm = pl.BlockSpec(memory_space=pl.ANY)
    return pl.pallas_call(
        kernel,
        out_shape=jax.ShapeDtypeStruct((requests, H * DH), BF16),
        in_specs=[smem, smem, vmem, vmem, hbm, hbm],
        out_specs=vmem,
        scratch_shapes=[
            pltpu.VMEM((slots, block, columns), BF16),
            pltpu.VMEM((slots, block, columns), BF16),
            pltpu.VMEM((xc, 1, 2 * LANES), F32),
            pltpu.VMEM((NZ, xc, LANES), BF16),
            pltpu.VMEM((NZ, xc, LANES), BF16),
            pltpu.VMEM((slots, G, KVH, DH), F32),
            pltpu.VMEM((KVH, 4, 4, DH), F32),
            pltpu.VMEM((KVH, 4, 1, LANES), F32),
            pltpu.VMEM((group, 4, DH), F32),
            pltpu.VMEM((group, 1, LANES), F32),
            pltpu.VMEM((NZ // 2, 8, DH), F32),
            pltpu.VMEM((NZ // 2, 1, LANES), F32),
            pltpu.SemaphoreType.DMA((2 * slots,)),
            pltpu.SemaphoreType.DMA((8,)),
            pltpu.SemaphoreType.DMA((8,)),
            pltpu.SemaphoreType.REGULAR,
        ],
        compiler_params=pltpu.CompilerParams(collective_id=0, has_side_effects=True),
        cost_estimate=pl.CostEstimate(
            flops=4 * slots * block * H * DH,
            bytes_accessed=4 * slots * block * columns,
            transcendentals=slots * block * H,
        ),
        name="decode",
    )(slot_request, slot_length, queries, new_kv, keys, values)


def solution(mesh):
    torus = Mesh(mesh.devices.reshape(mesh.shape["parts"], NX, NZ, NC), ("parts",) + SEQ)
    placed = (
        P("parts", SEQ),
        P("parts", SEQ),
        P(PARTS_SEQ, None, None),
        P(PARTS_SEQ, None, None),
        P(PARTS_SEQ),
        P(PARTS_SEQ),
    )
    return jax.shard_map(
        shards, mesh=torus, in_specs=placed, out_specs=P("parts", None), check_vma=False
    )
```

time: 241 us -> 82.3 us (0.34)
  blocking collectives: 155 us -> 0 us
  Pallas kernels: 0 us -> 80.6 us
  waiting for transfers between devices: 45.2 us -> 0 us
  other arithmetic: 19.3 us -> 0 us
  between operations: 13.6 us -> 0.01 us
  matrix products: 4.7 us -> 0 us
    all_gather x7 -> x0, blocking collectives: 155 us -> none  [the longest x6 143 us: gather_in_order(): tiles = lax.all_gather(tiles, axes[k])]
    pallas_call x0 -> x1, Pallas kernels: none -> 80.6 us  [shards(): pl.pallas_call(kernel, out_shape=jax.ShapeDtypeStruct((requests, H * DH),...]
    all_gather x2 -> x0, waiting for transfers between devices: 45.1 us -> none  [all_in_one(): both, at, found = (lax.all_gather(jnp.concatenate(lines), axis), 0, {})]
    exp x12 -> x0, other arithmetic: 8.41 us -> none  [the longest x10 7.04 us: combine_parts(): weight_second = jnp.exp(top_second - peak)]
    add x5 -> x0, other arithmetic: 6.2 us -> none  [the longest x2 4.41 us: combine_parts(): out_first * weight_first[..., None] + out_second * weight_second[..., None]]
    dot_general x5 -> x0, matrix products: 4.7 us -> none  [the longest x1 2.04 us: shards(): jnp.einsum('skgt,stkd->skgd', weights.astype(jnp.bfloat16), value_tiles,...]
  transfers between devices with their start and end apart: 2 -> 0, of which waited for: 2 -> 0; matrix products, arithmetic and copies ran while one was open for 0% -> 0% of each run, Pallas kernels for 0% -> 0%
where the time goes in v1:
time: 82.3 us; the launch traced here: 82.1 us
  Pallas kernels  80.6 us (98%)
  local copies, waits for them, and re-layouts  1.49 us (2%)
    pallas_call x1, Pallas kernels, shards(): pl.pallas_call(kernel, out_shape=jax.ShapeDtypeStruct((requests, H * DH),...  80.6 us

profile of v1, /device:TPU:65, one launch (start us, length us, event | category | flops | bytes accessed | tf_op | source)
XLA Modules:
  0.0 82.1 jit_solution(17670018922046986464)
XLA Ops:
  0.0 80.6 %decode.1 = bf16[4,8192]{1,0:T(4,128)(2,1)} custom-call(s32[2]{0:T(128)} %req_ref.1, s32[2]{0:T(128)} %len_ref.1, bf16[4,32]{1,0:T(4,128)(2,1)} %q_ref.1, bf16[4,8]{1,0:T(4,128)(2,1)} %kv_ref.1, bf16[2,512,1024]{2,1,0:T(8,128)(2,1)} %k_hbm.1, bf16[2,512,1024]{2,1,0:T(8,128)(2,1)} %v_hbm.1), custom_call_target="tpu_custom_call" | custom-call | flops 33554432 | bytes 4194304 | tf_op jit(solution)/shard_map/decode/pallas_call | solution.py:299
  80.6 1.5 %copy.8 = bf16[4,8192]{1,0:T(4,128)(2,1)} copy(bf16[4,8192]{1,0:T(4,128)(2,1)} %decode.1) | data formatting | bytes 131072

commit v2 on v1

v2 whole, which is shorter than its diff:
```python
import functools

import jax
import jax.numpy as jnp
from jax import lax
from jax.experimental import pallas as pl
from jax.experimental.pallas import tpu as pltpu
from jax.sharding import Mesh
from jax.sharding import PartitionSpec as P

H = 64
KVH = 8
DH = 128
G = H // KVH
LANES = 128
NX, NZ, NC = 8, 16, 2
AX, AZ, AC = "seq_0", "seq_1", "seq_2"
SEQ = (AX, AZ, AC)
PARTS_SEQ = ("parts", AX, AZ, AC)
NEG = -1e30
MESH = pl.DeviceIdType.MESH
F32, BF16 = jnp.float32, jnp.bfloat16
FAR_X = (4, 3, 5, 2, 6, 1, 7)
FAR_Z = (8, 7, 9, 6, 10, 5, 11, 4, 12, 3, 13, 2, 14, 1, 15)


def iota(shape, dim):
    return lax.broadcasted_iota(jnp.int32, shape, dim)


def at(x, z, c):
    return {AX: x, AZ: z, AC: c}


def wait_for(ref, sem):
    pltpu.make_async_copy(ref, ref, sem).wait()


def kernel(
    req_hbm, len_hbm, q_hbm, kv_hbm, k_hbm, v_hbm, out_ref,
    req_ref, len_ref, q_ref, kv_ref, kbuf, vbuf, above, below, g2, kv2, qscr, so, sml, ro, rml, ao, aml,
    load_sem, small_sem, send_sem, recv_sem, row_sem, x_sem, top_sem, pair_sem,
):
    x, z, c = lax.axis_index(AX), lax.axis_index(AZ), lax.axis_index(AC)
    requests, width = q_ref.shape
    new_width = kv_ref.shape[1]
    slots, block = k_hbm.shape[0], k_hbm.shape[1]
    xc = NX * NC
    zh, zl = z // 2, z % 2
    mine_d = c * 2 + zl
    mine = x * 4 + mine_d
    scale = DH**-0.5

    top_z = NZ - 1
    small = [
        pltpu.make_async_copy(src, dst, small_sem.at[i])
        for i, (src, dst) in enumerate(
            ((q_hbm, q_ref), (kv_hbm, kv_ref), (req_hbm, req_ref), (len_hbm, len_ref))
        )
    ]
    small[0].start()
    small[1].start()
    barrier = pltpu.get_barrier_semaphore()
    others = [(dx, dc) for dx in FAR_X + (0,) for dc in range(NC) if dx or dc]

    def on_z(z_there):
        return at(x, z_there % NZ, c)

    def plane_mate(dx, dc, z_there):
        return at((x + dx) % NX, z_there % NZ, (c + dc) % NC)

    @pl.when((z > 0) & (z < top_z))
    def _():
        pl.semaphore_signal(barrier, 1, device_id=on_z(NZ), device_id_type=MESH)

    @pl.when(z == 1)
    def _():
        pl.semaphore_signal(barrier, 1, device_id=at(x, z, 1 - c), device_id_type=MESH)

    @pl.when(z == 0)
    def _():
        for dx, dc in others + [(0, 0)]:
            there = plane_mate(dx, dc, top_z)
            pl.semaphore_signal(barrier, 1, device_id=there, device_id_type=MESH)

    for i in FAR_Z:

        @pl.when((z > 0) & (z + i < NZ))
        def _(i=i):
            pl.semaphore_signal(barrier, 1, device_id=on_z(z + i), device_id_type=MESH)

    @pl.when((z > 0) & (z + 2 < NZ))
    def _():
        for dx, dc in others:
            there = plane_mate(dx, dc, z + 2)
            pl.semaphore_signal(barrier, 1, device_id=there, device_id_type=MESH)

    loads = []
    for s in range(slots):
        loads.append(pltpu.make_async_copy(k_hbm.at[s], kbuf.at[s], load_sem.at[s]))
    for s in range(slots):
        loads.append(pltpu.make_async_copy(v_hbm.at[s], vbuf.at[s], load_sem.at[slots + s]))
    for load in small[2:] + loads:
        load.start()

    def as_row(ref, n):
        spread = (iota((n, LANES), 0) == iota((n, LANES), 1) % n).astype(BF16)
        wide = jnp.dot(ref[...], spread, preferred_element_type=F32)
        keep = iota((requests, LANES), 0) == iota((requests, LANES), 1) // n
        return jnp.sum(jnp.where(keep, wide, 0.0), axis=0, keepdims=True)

    place_z = zl * G + zh
    small[0].wait()
    small[1].wait()
    own = jnp.concatenate([as_row(q_ref, width), as_row(kv_ref, new_width)], axis=1)[None]
    above[pl.ds(place_z, 1)] = own

    def send(src, dst, phase, there, recv=None):
        pltpu.make_async_remote_copy(
            src_ref=src,
            dst_ref=dst,
            send_sem=send_sem.at[phase],
            recv_sem=recv_sem.at[phase] if recv is None else recv,
            device_id=there,
            device_id_type=MESH,
        ).start()

    greeted = z - 1 + jnp.where(z > 2, xc - 1, 0)
    greeted = greeted + jnp.where(z == top_z, xc, 0)
    pl.semaphore_wait(barrier, jnp.where(z == 0, NZ - 2, jnp.where(z == 1, 1, greeted)))

    row = above.at[place_z]

    def greeter(i):
        if i == 1:
            return z > 1
        return (z > i) | (z == 0) if i < top_z else (z == 0) | (z == top_z)

    for i in FAR_Z:

        @pl.when(greeter(i))
        def _(i=i):
            send(row, row, 8 + i, on_z(z + NZ - i), row_sem.at[z])

    @pl.when(z > 2)
    def _():
        pl.semaphore_signal(x_sem, 1, device_id=on_z(z + NZ - 2), device_id_type=MESH)

    @pl.when(z == top_z)
    def _():
        pl.semaphore_signal(x_sem, 1, device_id=on_z(NZ), device_id_type=MESH)

    @pl.when(z >= top_z - 1)
    def _():
        for dx, dc in others + [(0, 0)]:
            there = plane_mate(dx, dc, z + NZ - 2)
            pl.semaphore_signal(top_sem, 1, device_id=there, device_id_type=MESH)

    @pl.when((z == 1) | (z == 2))
    def _():
        below[...] = jnp.zeros_like(below)

    @pl.when((z > 0) & (z < top_z))
    def _():
        wait_for(row, row_sem.at[z + 1])
        send(row, row, 8 + NZ, on_z(z + 1), row_sem.at[z])

    @pl.when(z > 2)
    def _():
        wait_for(below, recv_sem.at[0])

    @pl.when(z > 1)
    def _():
        wait_for(row, row_sem.at[z - 1])
        below_z = (1 - zl) * G + (z - 1) // 2
        below[pl.ds(below_z, 1)] = above[pl.ds(below_z, 1)]

    @pl.when(z > 0)
    def _():
        below[pl.ds(place_z, 1)] = own

    @pl.when(z == top_z - 1)
    def _():
        wait_for(row, row_sem.at[0])
        send(below, below, 8, on_z(NZ), recv_sem.at[0])

    @pl.when((z > 0) & (z < top_z - 1))
    def _():
        wait_for(row, row_sem.at[z + 2])
        send(below, below, 0, on_z(z + 2), recv_sem.at[0])

    @pl.when(z == 0)
    def _():
        wait_for(row, row_sem.at[top_z])
        send(row, row, 9, on_z(top_z), row_sem.at[0])
        wait_for(below, recv_sem.at[0])

    small[2].wait()
    small[3].wait()
    req = [req_ref[s] for s in range(slots)]
    length = [len_ref[s] for s in range(slots)]
    lane512 = iota((LANES, 2 * NC * LANES), 1)
    sub512 = iota((LANES, 2 * NC * LANES), 0)
    place = []
    for cc in range(NC):
        m = lane512 % LANES
        want = jnp.where((lane512 // LANES) % 2 == 0, req[0], req[1]) * width + m % width
        piece = (lane512 // (2 * LANES)) * NC + cc
        place.append(((sub512 == want) & (m // width == piece)).astype(BF16))

    for i in range(3, NZ):

        @pl.when((z > 0) & (z + i < NZ))
        def _(i=i):
            wait_for(row, row_sem.at[z + i])

    @pl.when((z > 0) & (z != top_z - 1))
    def _():
        wait_for(row, row_sem.at[0])

    @pl.when((z >= top_z - 3) & (z < top_z - 1))
    def _():
        pl.semaphore_wait(top_sem, xc)
        pl.semaphore_signal(x_sem, 1, device_id=on_z(z + 2), device_id_type=MESH)

    z_of = iota((NZ, 2 * LANES), 0)
    z_of = 2 * (z_of % G) + z_of // G
    from_below = (z_of > 0) & (z_of < jnp.where(z == 0, top_z, z))
    rows = jnp.where(from_below, below[:, 0, :], above[:, 0, :]).astype(BF16)
    row1 = c * NX + x
    g2[pl.ds(row1, 1)] = rows[:, 0:LANES][None]
    kv2[pl.ds(row1, 1)] = rows[:, LANES : 2 * LANES][None]

    pl.semaphore_wait(x_sem, 1)
    for dx, dc in others:
        send(g2.at[row1], g2.at[row1], 1, plane_mate(dx, dc, z))
    for dx, dc in others:
        send(kv2.at[row1], kv2.at[row1], 2, plane_mate(dx, dc, z))
    pl.semaphore_signal(pair_sem, 1, device_id=at(x, 2 * zh + 1 - zl, c), device_id_type=MESH)
    for load in loads:
        load.wait()
    wait_for(g2.at[pl.ds(0, xc - 1)], recv_sem.at[1])

    picked = [None, None]
    for cc in range(NC):
        lhs = g2[cc * NX : (cc + 1) * NX].reshape(NX * NZ, LANES)
        placed = jnp.dot(lhs, place[cc], preferred_element_type=F32).reshape(NX, NZ, 4 * LANES)
        for s in range(slots):
            for zp in range(2):
                at_lane = (zp * 2 + s) * LANES
                part = placed[:, zp * G : (zp + 1) * G, at_lane : at_lane + LANES]
                picked[s] = part if picked[s] is None else picked[s] + part
    for s in range(slots):
        qscr[s] = picked[s].astype(BF16)
    pl.semaphore_wait(pair_sem, 1)

    lane = iota((G, LANES), 1)
    lane_s, lane_hh, lane_r = (lane // 8) % 2, (lane // 4) % 2, lane % 4
    inside = [iota((G, block), 1) < length[s] for s in range(slots)]
    order = FAR_X + (0,)
    weights, vals = {}, {}
    for n, dx in enumerate(order):
        k = (x + dx) % NX
        cols = pl.ds(pl.multiple_of(k * DH, DH), DH)
        tops, sums = [], []
        for s in range(slots):
            qk = qscr[s, k]
            sc = lax.dot_general(
                qk, kbuf[s, :, cols], (((1,), (1,)), ((), ())), preferred_element_type=F32
            )
            sc = jnp.where(inside[s], sc * scale, NEG)
            top = jnp.max(sc, axis=1, keepdims=True)
            w = jnp.exp(sc - top)
            tops.append(top)
            sums.append(jnp.sum(w, axis=1, keepdims=True))
            weights[n, s] = w.astype(BF16)
        of_slot = [
            jnp.where(
                lane < 64,
                jnp.where(lane_r == req[s], tops[s], NEG),
                jnp.where(lane_r == req[s], sums[s], 0.0),
            )
            for s in range(slots)
        ]
        vals[n] = jnp.where(lane_s == 0, of_slot[0], of_slot[1])
    for n, dx in enumerate(order):
        k = (x + dx) % NX
        cols = pl.ds(pl.multiple_of(k * DH, DH), DH)
        for d in range(4):
            sml[n, d] = jnp.where(
                lane_hh[0:1] == 0, vals[n][2 * d : 2 * d + 1], vals[n][2 * d + 1 : 2 * d + 2]
            )
        for s in range(slots):
            o = jnp.dot(weights[n, s], vbuf[s, :, cols], preferred_element_type=F32)
            for d in range(4):
                so[n, d, 2 * s : 2 * s + 2, :] = o[2 * d : 2 * d + 2]
        for dd in range(4):
            if dx or dd:
                d = dd if dx else (mine_d + dd) % 4
                there = at(k, 2 * zh + d % 2, d // 2)
                send(sml.at[n, d], rml.at[mine], 4, there)
                send(so.at[n, d], ro.at[mine], 3, there)
    last = len(order) - 1
    ro[pl.ds(mine, 1)] = so[last, pl.ds(mine_d, 1)]
    rml[pl.ds(mine, 1)] = sml[last, pl.ds(mine_d, 1)]

    wait_for(kv2.at[pl.ds(0, xc - 1)], recv_sem.at[2])
    total_rows = NZ * xc
    u, col = iota((2 * xc, total_rows), 0), iota((2 * xc, total_rows), 1)
    zi = (u % xc) // NC
    from_row = (u % NC) * NX + x // 2 + (NX // 2) * (u // xc)
    source = from_row * NZ + (zi % 2) * G + (x % 2) * (G // 2) + zi // 2
    pick = (col == source).astype(BF16)
    new = jnp.dot(pick, kv2[...].reshape(total_rows, LANES), preferred_element_type=F32)
    wide_l, wide_m = iota((LANES, requests * LANES), 0), iota((LANES, requests * LANES), 1)
    wide_r, wide_m = wide_m // LANES, wide_m % LANES
    to_new = (wide_l == wide_r * new_width + wide_m % new_width).astype(BF16)
    to_q = (wide_l == wide_r * width + wide_m % width).astype(BF16)
    new = jnp.dot(new.astype(BF16), to_new, preferred_element_type=F32)
    keep = (iota(new.shape, 1) % LANES) // new_width == iota(new.shape, 0) % xc
    new = jnp.where(keep, new, 0.0)

    def by_request(flat):
        return [flat[:, r * LANES : (r + 1) * LANES] for r in range(requests)]

    new_k = by_request(jnp.sum(new[0:xc], axis=0, keepdims=True))
    new_v = by_request(jnp.sum(new[xc : 2 * xc], axis=0, keepdims=True))
    u, col = iota((16, total_rows), 0), iota((16, total_rows), 1)
    source = ((u % NC) * NX + x) * NZ + ((u % 4) // NC) * G + 4 * c + u // 4
    pick = (col == source).astype(BF16)
    own_q = jnp.dot(pick, g2[...].reshape(total_rows, LANES), preferred_element_type=F32)
    own_q = jnp.dot(own_q.astype(BF16), to_q, preferred_element_type=F32)
    keep = (iota(own_q.shape, 1) % LANES) // width == iota(own_q.shape, 0) % 4
    own_q = jnp.where(keep, own_q, 0.0)
    k_rows = jnp.concatenate(new_k + new_k, axis=0)
    v_rows = jnp.concatenate(new_v + new_v, axis=0)
    new_score = []
    for half in range(2):
        q_rows = []
        for hh in range(2):
            i = (half * 2 + hh) * 4
            q_rows += by_request(jnp.sum(own_q[i : i + 4], axis=0, keepdims=True))
        q_rows = jnp.concatenate(q_rows, axis=0)
        new_score.append(jnp.sum(q_rows * k_rows, axis=1, keepdims=True) * scale)

    group = 4 * NX
    wait_for(rml.at[pl.ds(0, group - 1)], recv_sem.at[4])
    ml = rml[:, 0, :]
    top = jnp.max(ml, axis=0, keepdims=True)
    top = jnp.maximum(top, pltpu.roll(top, 8, 1))
    w = jnp.exp(ml - top)
    total = jnp.sum(w * pltpu.roll(ml, 64, 1), axis=0, keepdims=True)
    total = total + pltpu.roll(total, 8, 1)
    lane1 = iota((1, LANES), 1)
    aml[pl.ds(z, 1)] = jnp.where(lane1 < 64, top, pltpu.roll(total, 64, 1))[None]
    wait_for(ro.at[pl.ds(0, group - 1)], recv_sem.at[3])
    merged = []
    for hh in range(2):
        planes = [ro[:, s * 2 + hh, :] for s in range(slots)]
        for r in range(requests):
            acc = None
            for s in range(slots):
                i = 16 + s * 8 + hh * 4 + r
                part = w[:, i : i + 1] * planes[s]
                acc = part if acc is None else acc + part
            merged.append(jnp.sum(acc, axis=0, keepdims=True))
    ao[pl.ds(z, 1)] = jnp.concatenate(merged, axis=0)[None]

    for i in range(NZ):

        @pl.when(z != i)
        def _(i=i):
            send(aml.at[z], aml.at[z], 6, on_z(i))
            send(ao.at[z], ao.at[z], 5, on_z(i))

    wait_for(aml.at[pl.ds(0, NZ - 1)], recv_sem.at[6])
    sub = iota((8, LANES), 0)
    lane8 = iota((8, LANES), 1)
    m_at, l_at = lane8 == 16 + sub, lane8 == 80 + sub
    ways = []
    for half in range(2):
        planes = range(half, NZ, 2)
        ms = [jnp.sum(jnp.where(m_at, aml[i], 0.0), axis=1, keepdims=True) for i in planes]
        ls = [jnp.sum(jnp.where(l_at, aml[i], 0.0), axis=1, keepdims=True) for i in planes]
        peak = functools.reduce(jnp.maximum, ms, new_score[half])
        new_w = jnp.exp(new_score[half] - peak)
        factors = [jnp.exp(m - peak) for m in ms]
        denom = new_w
        for factor, part in zip(factors, ls):
            denom = denom + factor * part
        ways.append((new_w, factors, denom))
    wait_for(ao.at[pl.ds(0, NZ - 1)], recv_sem.at[5])
    base = pl.multiple_of((x * NC + c) * 4 * DH, 4 * DH)
    for half in range(2):
        new_w, factors, denom = ways[half]
        numer = new_w * v_rows
        for i, factor in zip(range(half, NZ, 2), factors):
            numer = numer + factor * ao[i]
        final = (numer / denom).astype(BF16)
        for hh in range(2):
            start = pl.multiple_of(base + (half * 2 + hh) * DH, DH)
            out_ref[:, pl.ds(start, DH)] = final[hh * 4 : hh * 4 + 4]

    here = out_ref.at[:, pl.ds(base, 4 * DH)]
    for dx, dc in others:
        send(here, here, 7, plane_mate(dx, dc, z))
    wait_for(out_ref.at[:, pl.ds(0, (xc - 1) * 4 * DH)], recv_sem.at[7])

    for i in range(1, NZ):

        @pl.when(greeter(i) if i > 1 else z != 1)
        def _(i=i):
            wait_for(row, send_sem.at[8 + i])

    @pl.when((z > 0) & (z < top_z))
    def _():
        wait_for(row, send_sem.at[8 + NZ])

    @pl.when((z > 0) & (z < top_z - 1))
    def _():
        wait_for(below, send_sem.at[0])

    @pl.when(z == top_z - 1)
    def _():
        wait_for(below, send_sem.at[8])

    wait_for(g2.at[pl.ds(0, xc - 1)], send_sem.at[1])
    wait_for(kv2.at[pl.ds(0, xc - 1)], send_sem.at[2])
    wait_for(ro.at[pl.ds(0, group - 1)], send_sem.at[3])
    wait_for(rml.at[pl.ds(0, group - 1)], send_sem.at[4])
    wait_for(ao.at[pl.ds(0, NZ - 1)], send_sem.at[5])
    wait_for(aml.at[pl.ds(0, NZ - 1)], send_sem.at[6])
    wait_for(out_ref.at[:, pl.ds(0, (xc - 1) * 4 * DH)], send_sem.at[7])


def shards(queries, new_kv, keys, values, slot_request, slot_length):
    slots, block, columns = keys.shape
    requests = queries.shape[0]
    xc, group = NX * NC, 4 * NX
    vmem = pl.BlockSpec(memory_space=pltpu.VMEM)
    hbm = pl.BlockSpec(memory_space=pl.ANY)
    return pl.pallas_call(
        kernel,
        out_shape=pltpu.VMEM((requests, H * DH), BF16),
        in_specs=[hbm] * 6,
        out_specs=vmem,
        scratch_shapes=[
            pltpu.SMEM(slot_request.shape, jnp.int32),
            pltpu.SMEM(slot_length.shape, jnp.int32),
            pltpu.VMEM(queries.shape, BF16),
            pltpu.VMEM(new_kv.shape, BF16),
            pltpu.VMEM((slots, block, columns), BF16),
            pltpu.VMEM((slots, block, columns), BF16),
            pltpu.VMEM((NZ, 1, 2 * LANES), F32),
            pltpu.VMEM((NZ, 1, 2 * LANES), F32),
            pltpu.VMEM((xc, NZ, LANES), BF16),
            pltpu.VMEM((xc, NZ, LANES), BF16),
            pltpu.VMEM((slots, KVH, G, DH), BF16),
            pltpu.VMEM((KVH, 4, 4, DH), F32),
            pltpu.VMEM((KVH, 4, 1, LANES), F32),
            pltpu.VMEM((group, 4, DH), F32),
            pltpu.VMEM((group, 1, LANES), F32),
            pltpu.VMEM((NZ, 8, DH), F32),
            pltpu.VMEM((NZ, 1, LANES), F32),
            pltpu.SemaphoreType.DMA((2 * slots,)),
            pltpu.SemaphoreType.DMA((4,)),
            pltpu.SemaphoreType.DMA((9 + NZ,)),
            pltpu.SemaphoreType.DMA((8,)),
            pltpu.SemaphoreType.DMA((NZ,)),
            pltpu.SemaphoreType.REGULAR,
            pltpu.SemaphoreType.REGULAR,
            pltpu.SemaphoreType.REGULAR,
        ],
        compiler_params=pltpu.CompilerParams(collective_id=0, has_side_effects=True),
        cost_estimate=pl.CostEstimate(
            flops=4 * slots * block * H * DH,
            bytes_accessed=4 * slots * block * columns,
            transcendentals=slots * block * H,
        ),
        name="decode",
    )(slot_request, slot_length, queries, new_kv, keys, values)


def solution(mesh):
    torus = Mesh(mesh.devices.reshape(mesh.shape["parts"], NX, NZ, NC), ("parts",) + SEQ)
    placed = (
        P("parts", SEQ),
        P("parts", SEQ),
        P(PARTS_SEQ, None, None),
        P(PARTS_SEQ, None, None),
        P(PARTS_SEQ),
        P(PARTS_SEQ),
    )
    return jax.shard_map(
        shards, mesh=torus, in_specs=placed, out_specs=P("parts", None), check_vma=False
    )
```

time: 82.3 us -> 76.8 us (0.933)
  Pallas kernels: 80.6 us -> 76 us
  local copies, waits for them, and re-layouts: 1.49 us -> 0.63 us
    pallas_call x1, Pallas kernels: 80.6 us -> 76 us  [shards(): pl.pallas_call(kernel, out_shape=pltpu.VMEM((requests, H * DH), BF16), in...]
    unnamed x1, local copies, waits for them, and re-layouts: 1.49 us -> 0.63 us
where the time goes in v2:
time: 76.8 us; the launch traced here: 76.7 us
  Pallas kernels  76 us (99%)
    pallas_call x1, Pallas kernels, shards(): pl.pallas_call(kernel, out_shape=pltpu.VMEM((requests, H * DH), BF16), in...  76 us

profile of v2, /device:TPU:65, one launch (start us, length us, event | category | flops | bytes accessed | tf_op | source)
XLA Modules:
  0.0 76.7 jit_solution(895728487266942088)
XLA Ops:
  0.0 76.0 %decode.1 = bf16[4,8192]{1,0:T(4,128)(2,1)S(1)} custom-call(s32[2]{0:T(128)} %req_hbm.1, s32[2]{0:T(128)} %len_hbm.1, bf16[4,32]{1,0:T(4,128)(2,1)} %q_hbm.1, bf16[4,8]{1,0:T(4,128)(2,1)} %kv_hbm.1, bf16[2,512,1024]{2,1,0:T(8,128)(2,1)} %k_hbm.1, bf16[2,512,1024]{2,1,0:T(8,128)(2,1)} %v_hbm.1), custom_call_target="tpu_custom_call" | custom-call | flops 33554432 | bytes 4194304 | tf_op jit(solution)/shard_map/decode/pallas_call | solution.py:442
  76.1 0.6 copy.8

commit v3 on v2

--- a/solution.py
+++ b/solution.py
@@ -234,8 +234,6 @@
     pl.semaphore_wait(x_sem, 1)
     for dx, dc in others:
         send(g2.at[row1], g2.at[row1], 1, plane_mate(dx, dc, z))
-    for dx, dc in others:
-        send(kv2.at[row1], kv2.at[row1], 2, plane_mate(dx, dc, z))
     pl.semaphore_signal(pair_sem, 1, device_id=at(x, 2 * zh + 1 - zl, c), device_id_type=MESH)
     for load in loads:
         load.wait()
@@ -259,89 +257,55 @@
     inside = [iota((G, block), 1) < length[s] for s in range(slots)]
     order = FAR_X + (0,)
     weights, vals = {}, {}
-    for n, dx in enumerate(order):
-        k = (x + dx) % NX
-        cols = pl.ds(pl.multiple_of(k * DH, DH), DH)
-        tops, sums = [], []
-        for s in range(slots):
-            qk = qscr[s, k]
-            sc = lax.dot_general(
-                qk, kbuf[s, :, cols], (((1,), (1,)), ((), ())), preferred_element_type=F32
-            )
-            sc = jnp.where(inside[s], sc * scale, NEG)
-            top = jnp.max(sc, axis=1, keepdims=True)
-            w = jnp.exp(sc - top)
-            tops.append(top)
-            sums.append(jnp.sum(w, axis=1, keepdims=True))
-            weights[n, s] = w.astype(BF16)
-        of_slot = [
-            jnp.where(
-                lane < 64,
-                jnp.where(lane_r == req[s], tops[s], NEG),
-                jnp.where(lane_r == req[s], sums[s], 0.0),
-            )
-            for s in range(slots)
-        ]
-        vals[n] = jnp.where(lane_s == 0, of_slot[0], of_slot[1])
-    for n, dx in enumerate(order):
-        k = (x + dx) % NX
-        cols = pl.ds(pl.multiple_of(k * DH, DH), DH)
-        for d in range(4):
-            sml[n, d] = jnp.where(
-                lane_hh[0:1] == 0, vals[n][2 * d : 2 * d + 1], vals[n][2 * d + 1 : 2 * d + 2]
-            )
-        for s in range(slots):
-            o = jnp.dot(weights[n, s], vbuf[s, :, cols], preferred_element_type=F32)
+    numbered = list(enumerate(order))
+    for part in (numbered[0:3], numbered[3:]):
+        for n, dx in part:
+            k = (x + dx) % NX
+            cols = pl.ds(pl.multiple_of(k * DH, DH), DH)
+            tops, sums = [], []
+            for s in range(slots):
+                qk = qscr[s, k]
+                sc = lax.dot_general(
+                    qk, kbuf[s, :, cols], (((1,), (1,)), ((), ())), preferred_element_type=F32
+                )
+                sc = jnp.where(inside[s], sc * scale, NEG)
+                top = jnp.max(sc, axis=1, keepdims=True)
+                w = jnp.exp(sc - top)
+                tops.append(top)
+                sums.append(jnp.sum(w, axis=1, keepdims=True))
+                weights[n, s] = w.astype(BF16)
+            of_slot = [
+                jnp.where(
+                    lane < 64,
+                    jnp.where(lane_r == req[s], tops[s], NEG),
+                    jnp.where(lane_r == req[s], sums[s], 0.0),
+                )
+                for s in range(slots)
+            ]
+            vals[n] = jnp.where(lane_s == 0, of_slot[0], of_slot[1])
+        for n, dx in part:
+            k = (x + dx) % NX
+            cols = pl.ds(pl.multiple_of(k * DH, DH), DH)
             for d in range(4):
-                so[n, d, 2 * s : 2 * s + 2, :] = o[2 * d : 2 * d + 2]
-        for dd in range(4):
-            if dx or dd:
-                d = dd if dx else (mine_d + dd) % 4
-                there = at(k, 2 * zh + d % 2, d // 2)
-                send(sml.at[n, d], rml.at[mine], 4, there)
-                send(so.at[n, d], ro.at[mine], 3, there)
+                sml[n, d] = jnp.where(
+                    lane_hh[0:1] == 0, vals[n][2 * d : 2 * d + 1], vals[n][2 * d + 1 : 2 * d + 2]
+                )
+            for s in range(slots):
+                o = jnp.dot(weights[n, s], vbuf[s, :, cols], preferred_element_type=F32)
+                for d in range(4):
+                    so[n, d, 2 * s : 2 * s + 2, :] = o[2 * d : 2 * d + 2]
+            for dd in range(4):
+                if dx or dd:
+                    d = dd if dx else (mine_d + dd) % 4
+                    there = at(k, 2 * zh + d % 2, d // 2)
+                    send(sml.at[n, d], rml.at[mine], 4, there)
+                    send(so.at[n, d], ro.at[mine], 3, there)
     last = len(order) - 1
     ro[pl.ds(mine, 1)] = so[last, pl.ds(mine_d, 1)]
     rml[pl.ds(mine, 1)] = sml[last, pl.ds(mine_d, 1)]
 
-    wait_for(kv2.at[pl.ds(0, xc - 1)], recv_sem.at[2])
-    total_rows = NZ * xc
-    u, col = iota((2 * xc, total_rows), 0), iota((2 * xc, total_rows), 1)
-    zi = (u % xc) // NC
-    from_row = (u % NC) * NX + x // 2 + (NX // 2) * (u // xc)
-    source = from_row * NZ + (zi % 2) * G + (x % 2) * (G // 2) + zi // 2
-    pick = (col == source).astype(BF16)
-    new = jnp.dot(pick, kv2[...].reshape(total_rows, LANES), preferred_element_type=F32)
-    wide_l, wide_m = iota((LANES, requests * LANES), 0), iota((LANES, requests * LANES), 1)
-    wide_r, wide_m = wide_m // LANES, wide_m % LANES
-    to_new = (wide_l == wide_r * new_width + wide_m % new_width).astype(BF16)
-    to_q = (wide_l == wide_r * width + wide_m % width).astype(BF16)
-    new = jnp.dot(new.astype(BF16), to_new, preferred_element_type=F32)
-    keep = (iota(new.shape, 1) % LANES) // new_width == iota(new.shape, 0) % xc
-    new = jnp.where(keep, new, 0.0)
-
-    def by_request(flat):
-        return [flat[:, r * LANES : (r + 1) * LANES] for r in range(requests)]
-
-    new_k = by_request(jnp.sum(new[0:xc], axis=0, keepdims=True))
-    new_v = by_request(jnp.sum(new[xc : 2 * xc], axis=0, keepdims=True))
-    u, col = iota((16, total_rows), 0), iota((16, total_rows), 1)
-    source = ((u % NC) * NX + x) * NZ + ((u % 4) // NC) * G + 4 * c + u // 4
-    pick = (col == source).astype(BF16)
-    own_q = jnp.dot(pick, g2[...].reshape(total_rows, LANES), preferred_element_type=F32)
-    own_q = jnp.dot(own_q.astype(BF16), to_q, preferred_element_type=F32)
-    keep = (iota(own_q.shape, 1) % LANES) // width == iota(own_q.shape, 0) % 4
-    own_q = jnp.where(keep, own_q, 0.0)
-    k_rows = jnp.concatenate(new_k + new_k, axis=0)
-    v_rows = jnp.concatenate(new_v + new_v, axis=0)
-    new_score = []
-    for half in range(2):
-        q_rows = []
-        for hh in range(2):
-            i = (half * 2 + hh) * 4
-            q_rows += by_request(jnp.sum(own_q[i : i + 4], axis=0, keepdims=True))
-        q_rows = jnp.concatenate(q_rows, axis=0)
-        new_score.append(jnp.sum(q_rows * k_rows, axis=1, keepdims=True) * scale)
+    for dx, dc in others:
+        send(kv2.at[row1], kv2.at[row1], 2, plane_mate(dx, dc, z))
 
     group = 4 * NX
     wait_for(rml.at[pl.ds(0, group - 1)], recv_sem.at[4])
@@ -372,6 +336,45 @@
         def _(i=i):
             send(aml.at[z], aml.at[z], 6, on_z(i))
             send(ao.at[z], ao.at[z], 5, on_z(i))
+
+    wait_for(kv2.at[pl.ds(0, xc - 1)], recv_sem.at[2])
+    total_rows = NZ * xc
+    u, col = iota((2 * xc, total_rows), 0), iota((2 * xc, total_rows), 1)
+    zi = (u % xc) // NC
+    from_row = (u % NC) * NX + x // 2 + (NX // 2) * (u // xc)
+    source = from_row * NZ + (zi % 2) * G + (x % 2) * (G // 2) + zi // 2
+    pick = (col == source).astype(BF16)
+    new = jnp.dot(pick, kv2[...].reshape(total_rows, LANES), preferred_element_type=F32)
+    wide_l, wide_m = iota((LANES, requests * LANES), 0), iota((LANES, requests * LANES), 1)
+    wide_r, wide_m = wide_m // LANES, wide_m % LANES
+    to_new = (wide_l == wide_r * new_width + wide_m % new_width).astype(BF16)
+    to_q = (wide_l == wide_r * width + wide_m % width).astype(BF16)
+    new = jnp.dot(new.astype(BF16), to_new, preferred_element_type=F32)
+    keep = (iota(new.shape, 1) % LANES) // new_width == iota(new.shape, 0) % xc
+    new = jnp.where(keep, new, 0.0)
+
+    def by_request(flat):
+        return [flat[:, r * LANES : (r + 1) * LANES] for r in range(requests)]
+
+    new_k = by_request(jnp.sum(new[0:xc], axis=0, keepdims=True))
+    new_v = by_request(jnp.sum(new[xc : 2 * xc], axis=0, keepdims=True))
+    u, col = iota((16, total_rows), 0), iota((16, total_rows), 1)
+    source = ((u % NC) * NX + x) * NZ + ((u % 4) // NC) * G + 4 * c + u // 4
+    pick = (col == source).astype(BF16)
+    own_q = jnp.dot(pick, g2[...].reshape(total_rows, LANES), preferred_element_type=F32)
+    own_q = jnp.dot(own_q.astype(BF16), to_q, preferred_element_type=F32)
+    keep = (iota(own_q.shape, 1) % LANES) // width == iota(own_q.shape, 0) % 4
+    own_q = jnp.where(keep, own_q, 0.0)
+    k_rows = jnp.concatenate(new_k + new_k, axis=0)
+    v_rows = jnp.concatenate(new_v + new_v, axis=0)
+    new_score = []
+    for half in range(2):
+        q_rows = []
+        for hh in range(2):
+            i = (half * 2 + hh) * 4
+            q_rows += by_request(jnp.sum(own_q[i : i + 4], axis=0, keepdims=True))
+        q_rows = jnp.concatenate(q_rows, axis=0)
+        new_score.append(jnp.sum(q_rows * k_rows, axis=1, keepdims=True) * scale)
 
     wait_for(aml.at[pl.ds(0, NZ - 1)], recv_sem.at[6])
     sub = iota((8, LANES), 0)

time: 76.8 us -> 76.2 us (level)
  no operation moved by 1% of the time
where the time goes in v3:
time: 76.2 us; the launch traced here: 76.1 us
  Pallas kernels  75.4 us (99%)
    pallas_call x1, Pallas kernels, shards(): pl.pallas_call(kernel, out_shape=pltpu.VMEM((requests, H * DH), BF16), in...  75.4 us

profile of v3, /device:TPU:65, one launch (start us, length us, event | category | flops | bytes accessed | tf_op | source)
XLA Modules:
  0.0 76.1 jit_solution(13455314483626289534)
XLA Ops:
  0.0 75.4 %decode.1 = bf16[4,8192]{1,0:T(4,128)(2,1)S(1)} custom-call(s32[2]{0:T(128)} %req_hbm.1, s32[2]{0:T(128)} %len_hbm.1, bf16[4,32]{1,0:T(4,128)(2,1)} %q_hbm.1, bf16[4,8]{1,0:T(4,128)(2,1)} %kv_hbm.1, bf16[2,512,1024]{2,1,0:T(8,128)(2,1)} %k_hbm.1, bf16[2,512,1024]{2,1,0:T(8,128)(2,1)} %v_hbm.1), custom_call_target="tpu_custom_call" | custom-call | flops 33554432 | bytes 4194304 | tf_op jit(solution)/shard_map/decode/pallas_call | solution.py:445
  75.4 0.6 copy.8

commit v4 on v3

--- a/solution.py
+++ b/solution.py
@@ -290,10 +290,13 @@
                 sml[n, d] = jnp.where(
                     lane_hh[0:1] == 0, vals[n][2 * d : 2 * d + 1], vals[n][2 * d + 1 : 2 * d + 2]
                 )
-            for s in range(slots):
-                o = jnp.dot(weights[n, s], vbuf[s, :, cols], preferred_element_type=F32)
-                for d in range(4):
-                    so[n, d, 2 * s : 2 * s + 2, :] = o[2 * d : 2 * d + 2]
+            o = [
+                jnp.dot(weights[n, s], vbuf[s, :, cols], preferred_element_type=F32)
+                for s in range(slots)
+            ]
+            for d in range(4):
+                four = jnp.concatenate([o[s][2 * d : 2 * d + 2] for s in range(slots)], axis=0)
+                so[n, d] = four.astype(BF16)
             for dd in range(4):
                 if dx or dd:
                     d = dd if dx else (mine_d + dd) % 4
@@ -318,9 +321,10 @@
     lane1 = iota((1, LANES), 1)
     aml[pl.ds(z, 1)] = jnp.where(lane1 < 64, top, pltpu.roll(total, 64, 1))[None]
     wait_for(ro.at[pl.ds(0, group - 1)], recv_sem.at[3])
+    got = ro[...].astype(F32)
     merged = []
     for hh in range(2):
-        planes = [ro[:, s * 2 + hh, :] for s in range(slots)]
+        planes = [got[:, s * 2 + hh, :] for s in range(slots)]
         for r in range(requests):
             acc = None
             for s in range(slots):
@@ -328,7 +332,7 @@
                 part = w[:, i : i + 1] * planes[s]
                 acc = part if acc is None else acc + part
             merged.append(jnp.sum(acc, axis=0, keepdims=True))
-    ao[pl.ds(z, 1)] = jnp.concatenate(merged, axis=0)[None]
+    ao[pl.ds(z, 1)] = jnp.concatenate(merged, axis=0).astype(BF16)[None]
 
     for i in range(NZ):
 
@@ -398,7 +402,7 @@
         new_w, factors, denom = ways[half]
         numer = new_w * v_rows
         for i, factor in zip(range(half, NZ, 2), factors):
-            numer = numer + factor * ao[i]
+            numer = numer + factor * ao[i].astype(F32)
         final = (numer / denom).astype(BF16)
         for hh in range(2):
             start = pl.multiple_of(base + (half * 2 + hh) * DH, DH)
@@ -459,11 +463,11 @@
             pltpu.VMEM((xc, NZ, LANES), BF16),
             pltpu.VMEM((xc, NZ, LANES), BF16),
             pltpu.VMEM((slots, KVH, G, DH), BF16),
-            pltpu.VMEM((KVH, 4, 4, DH), F32),
+            pltpu.VMEM((KVH, 4, 4, DH), BF16),
             pltpu.VMEM((KVH, 4, 1, LANES), F32),
-            pltpu.VMEM((group, 4, DH), F32),
+            pltpu.VMEM((group, 4, DH), BF16),
             pltpu.VMEM((group, 1, LANES), F32),
-            pltpu.VMEM((NZ, 8, DH), F32),
+            pltpu.VMEM((NZ, 8, DH), BF16),
             pltpu.VMEM((NZ, 1, LANES), F32),
             pltpu.SemaphoreType.DMA((2 * slots,)),
             pltpu.SemaphoreType.DMA((4,)),

time: 76.2 us -> 75.6 us (level)
  no operation moved by 1% of the time
where the time goes in v4:
time: 75.6 us; the launch traced here: 75.5 us
  Pallas kernels  74.9 us (99%)
    pallas_call x1, Pallas kernels, shards(): pl.pallas_call(kernel, out_shape=pltpu.VMEM((requests, H * DH), BF16), in...  74.9 us

profile of v4, /device:TPU:65, one launch (start us, length us, event | category | flops | bytes accessed | tf_op | source)
XLA Modules:
  0.0 75.5 jit_solution(421092106435133916)
XLA Ops:
  0.0 74.9 %decode.1 = bf16[4,8192]{1,0:T(4,128)(2,1)S(1)} custom-call(s32[2]{0:T(128)} %req_hbm.1, s32[2]{0:T(128)} %len_hbm.1, bf16[4,32]{1,0:T(4,128)(2,1)} %q_hbm.1, bf16[4,8]{1,0:T(4,128)(2,1)} %kv_hbm.1, bf16[2,512,1024]{2,1,0:T(8,128)(2,1)} %k_hbm.1, bf16[2,512,1024]{2,1,0:T(8,128)(2,1)} %v_hbm.1), custom_call_target="tpu_custom_call" | custom-call | flops 33554432 | bytes 4194304 | tf_op jit(solution)/shard_map/decode/pallas_call | solution.py:449
  74.9 0.6 copy.8

commit v5 on v4

--- a/solution.py
+++ b/solution.py
@@ -38,7 +38,7 @@
 
 def kernel(
     req_hbm, len_hbm, q_hbm, kv_hbm, k_hbm, v_hbm, out_ref,
-    req_ref, len_ref, q_ref, kv_ref, kbuf, vbuf, above, below, g2, kv2, qscr, so, sml, ro, rml, ao, aml,
+    req_ref, len_ref, q_ref, kv_ref, kbuf, vbuf, above, below, g2, kv2, qscr, so, sml, ro, got, rml, ao, aml,
     load_sem, small_sem, send_sem, recv_sem, row_sem, x_sem, top_sem, pair_sem,
 ):
     x, z, c = lax.axis_index(AX), lax.axis_index(AZ), lax.axis_index(AC)
@@ -321,7 +321,7 @@
     lane1 = iota((1, LANES), 1)
     aml[pl.ds(z, 1)] = jnp.where(lane1 < 64, top, pltpu.roll(total, 64, 1))[None]
     wait_for(ro.at[pl.ds(0, group - 1)], recv_sem.at[3])
-    got = ro[...].astype(F32)
+    got[...] = ro[...].astype(F32)
     merged = []
     for hh in range(2):
         planes = [got[:, s * 2 + hh, :] for s in range(slots)]
@@ -466,6 +466,7 @@
             pltpu.VMEM((KVH, 4, 4, DH), BF16),
             pltpu.VMEM((KVH, 4, 1, LANES), F32),
             pltpu.VMEM((group, 4, DH), BF16),
+            pltpu.VMEM((group, 4, DH), F32),
             pltpu.VMEM((group, 1, LANES), F32),
             pltpu.VMEM((NZ, 8, DH), BF16),
             pltpu.VMEM((NZ, 1, LANES), F32),

time: 75.6 us -> 75.6 us (level)
  no operation moved by 1% of the time
where the time goes in v5:
time: 75.6 us; the launch traced here: 75.5 us
  Pallas kernels  74.9 us (99%)
    pallas_call x1, Pallas kernels, shards(): pl.pallas_call(kernel, out_shape=pltpu.VMEM((requests, H * DH), BF16), in...  74.9 us

profile of v5, /device:TPU:65, one launch (start us, length us, event | category | flops | bytes accessed | tf_op | source)
XLA Modules:
  0.0 75.5 jit_solution(3030724140653266574)
XLA Ops:
  0.0 74.9 %decode.1 = bf16[4,8192]{1,0:T(4,128)(2,1)S(1)} custom-call(s32[2]{0:T(128)} %req_hbm.1, s32[2]{0:T(128)} %len_hbm.1, bf16[4,32]{1,0:T(4,128)(2,1)} %q_hbm.1, bf16[4,8]{1,0:T(4,128)(2,1)} %kv_hbm.1, bf16[2,512,1024]{2,1,0:T(8,128)(2,1)} %k_hbm.1, bf16[2,512,1024]{2,1,0:T(8,128)(2,1)} %v_hbm.1), custom_call_target="tpu_custom_call" | custom-call | flops 33554432 | bytes 4194304 | tf_op jit(solution)/shard_map/decode/pallas_call | solution.py:449
  74.9 0.6 copy.8
